TPU v7x, 128 devices: a whole 4x4x4 slice. The times are simulated.
128 devices in a mesh: tiles: 32 (over x, y, core), reps: 4 (over z).
Axes of the slice: x: 4, y: 4, z: 4, core: 2. Of those that a mesh axis runs over, the one named last changes fastest.
Arguments:
- tiles_w: bfloat16 [4096, 128, 128], P('tiles'), may hold values from 0.0001 to 4
- tile_worker: int32 [4096], P('tiles'), may hold values from 0 to 15
- tile_owner: int32 [4096], P('tiles'), may hold values from 0 to 31
- owner_block: int32 [32, 32], P('tiles'), may hold values from 0 to 1
- worker_base: float32 [65536], P('tiles'), may hold values from -6 to 6
- worker_noise: float32 [65536], P('tiles'), may hold values from 0.2 to 1.5
- worker_cluster: int32 [65536], P('tiles'), may hold values from 0 to 255
- firm_base: float32 [8192], P('tiles'), may hold values from -6 to 6
- firm_noise: float32 [8192], P('tiles'), may hold values from 0.2 to 1.5
- firm_cluster: int32 [8192], P('tiles'), may hold values from 0 to 255
- signs: int32 [256, 256], P('reps'), may hold values from 0 to 1
- covariates: float32 [8192, 512], P('tiles'), may hold values from -0.0625 to 0.0625
- whitening: float32 [512, 512], replicated, may hold values from -0.25 to 0.25
Outputs:
- worker_effect: float32 [256, 65536], P('reps', 'tiles')
- firm_effect: float32 [256, 8192], P('reps', 'tiles')
- coefficients: float32 [256, 512], P('reps')
- covariance: float32 [512, 512], P('tiles')
Inputs may be any that keep to these rules, and one draw needn't show every extreme that they name: `tile_worker`: local worker block of each tile. `tile_owner`: owner of each tile's firm block. `owner_block`: firm block among the owner's 2 blocks. `signs`: a bit that gives the sign 2 b - 1.
All inputs are finite; a program needn't handle non-finite values.
Results may differ from a plain program's by a relative error of at most 0.0023.
Values may be sent and summed in bfloat16 or wider, within the bound.
No kernel may reach another device: no remote copies, remote signals or barrier semaphores. Data moves between devices by JAX's collectives and lax.ppermute only.
A program may use at most 64 MiB of HBM per device.

v0:
```python
import jax
import jax.numpy as jnp
from jax import lax
from jax.sharding import PartitionSpec as P

WORK_BLOCKS = 16
FIRM_BLOCKS = 2
SWEEPS = 6
spectral_bound = 0.8


def chebyshev_weights(sweep_count):
    weights = [1.0]
    weights.append(1.0 / (1.0 - 0.5 * spectral_bound * spectral_bound))
    while len(weights) < sweep_count:
        weights.append(1.0 / (1.0 - 0.25 * spectral_bound * spectral_bound * weights[-1]))
    return weights


def one_hot_rows(indices, row_count):
    return (indices[None, :] == jnp.arange(row_count, dtype=jnp.int32)[:, None]).astype(jnp.float32)


def wild_outcome(base_value, noise_scale, cluster, flip_table):
    clusters_hot = (
        cluster[None, :] == jnp.arange(flip_table.shape[1], dtype=jnp.int32)[:, None]
    ).astype(jnp.bfloat16)
    flip_values = jnp.dot(flip_table, clusters_hot, preferred_element_type=jnp.float32)
    return base_value[None, :] + noise_scale[None, :] * flip_values


def body(
    tiles_w,
    tile_worker,
    tile_owner,
    owner_block,
    worker_base,
    worker_noise,
    worker_cluster,
    firm_base,
    firm_noise,
    firm_cluster,
    signs,
    covariates,
    whitening,
):
    highest = lax.Precision.HIGHEST
    owners_count = lax.axis_size("tiles")
    tile_cells = tiles_w.shape[1]
    replicas_here = signs.shape[0]
    flip_table = (2 * signs - 1).astype(jnp.bfloat16)
    worker_outcome = wild_outcome(worker_base, worker_noise, worker_cluster, flip_table).reshape(
        replicas_here, WORK_BLOCKS, tile_cells
    )
    firm_outcome = wild_outcome(firm_base, firm_noise, firm_cluster, flip_table).reshape(
        replicas_here, FIRM_BLOCKS, tile_cells
    )
    row_mass = jnp.sum(tiles_w, axis=2, dtype=jnp.float32)
    col_mass = jnp.sum(tiles_w, axis=1, dtype=jnp.float32)
    worker_hot = one_hot_rows(tile_worker, WORK_BLOCKS)
    worker_scale = 1.0 + jnp.einsum("bt,tw->bw", worker_hot, row_mass, precision=highest)
    owner_hot = one_hot_rows(tile_owner, owners_count)
    my_blocks = owner_block[0]
    tile_block = tile_owner * FIRM_BLOCKS + jnp.sum(
        jnp.where(owner_hot > 0, my_blocks[:, None], 0), axis=0
    )
    dense_hot = one_hot_rows(tile_block, owners_count * FIRM_BLOCKS)
    firm_mass = lax.psum_scatter(
        jnp.einsum("nt,tf->nf", dense_hot, col_mass, precision=highest),
        "tiles",
        scatter_dimension=0,
        tiled=True,
    )
    firm_scale = 1.0 + firm_mass
    omegas = chebyshev_weights(SWEEPS)
    firm_older = jnp.zeros((replicas_here, FIRM_BLOCKS, tile_cells), jnp.float32)
    firm_newer = firm_older
    firm_now = firm_older
    worker_now = worker_outcome
    tile_firm = None
    for sweep_index in range(SWEEPS):
        if sweep_index == 0:
            worker_now = worker_outcome
        else:
            pulled = jnp.einsum(
                "twf,rtf->rtw", tiles_w, tile_firm, preferred_element_type=jnp.float32
            )
            worker_sum = jnp.einsum("bt,rtw->rbw", worker_hot, pulled, precision=highest)
            worker_now = worker_outcome - worker_sum / worker_scale[None]
        worker_round = worker_now.astype(jnp.bfloat16)
        tile_values = jnp.take(worker_round, tile_worker, axis=1)
        pushed = jnp.einsum(
            "twf,rtw->rtf", tiles_w, tile_values, preferred_element_type=jnp.float32
        )
        firm_sum = lax.psum_scatter(
            jnp.einsum("nt,rtf->rnf", dense_hot, pushed, precision=highest),
            "tiles",
            scatter_dimension=1,
            tiled=True,
        )
        firm_target = firm_outcome - firm_sum / firm_scale[None]
        firm_now = firm_older + omegas[sweep_index] * (firm_target - firm_older)
        firm_older, firm_newer = (firm_newer, firm_now)
        if sweep_index + 1 < SWEEPS:
            firm_round = firm_now.astype(jnp.bfloat16)
            every_firm = lax.all_gather(firm_round, "tiles", axis=1, tiled=True)
            tile_firm = jnp.take(every_firm, tile_block, axis=1)
    worker_effect = worker_now.reshape(replicas_here, WORK_BLOCKS * tile_cells)
    firm_flat = firm_now.reshape(replicas_here, FIRM_BLOCKS * tile_cells)
    mixing = jnp.dot(covariates, whitening.T, precision=highest)
    local_term = jnp.dot(firm_flat, mixing, precision=highest)
    summed = lax.psum(local_term, "tiles")
    share_rows = summed.shape[1] // owners_count
    own_columns = lax.dynamic_slice_in_dim(
        summed, lax.axis_index("tiles") * share_rows, share_rows, 1
    )
    moment = jnp.dot(own_columns.T, summed, precision=highest)
    covariance = lax.psum(moment, "reps") / (replicas_here * lax.axis_size("reps"))
    return (worker_effect, firm_flat, summed, covariance)


def solution(mesh):
    placed = (
        P("tiles", None, None),
        P("tiles"),
        P("tiles"),
        P("tiles", None),
        P("tiles"),
        P("tiles"),
        P("tiles"),
        P("tiles"),
        P("tiles"),
        P("tiles"),
        P("reps", None),
        P("tiles", None),
        P(),
    )
    return jax.shard_map(
        body,
        mesh=mesh,
        in_specs=placed,
        out_specs=(P("reps", "tiles"), P("reps", "tiles"), P("reps", None), P("tiles", None)),
        check_vma=False,
    )
```

profile of v0, /device:TPU:6, one launch (start us, length us, event | category | flops | bytes accessed | tf_op | source)
XLA Modules:
  0.0 1033.3 jit_solution(7390925900868006559)
XLA Ops:
  12.5 4.1 convolution_bitcast_fusion.10
  16.6 4.2 fusion.56
  20.8 2.6 copy.89
  25.3 3.5 convert_reduce_fusion
  28.9 109.8 %all-reduce = f32[64,128]{1,0:T(8,128)S(1)} all-reduce(f32[64,128]{1,0:T(8,128)S(1)} %fusion.164), channel_id=3, replica_groups=mesh['tiles'=32,'reps'=4] {'tiles'}, use_global_device_ids=true, to_apply=%region_3.0.clone | all-reduce | flops 8192 | bytes 65536
  140.8 57.8 %all-gather.6.cloned.1.call-done = bf16[64,64,128]{2,0,1:T(8,128)(2,1)} async-done(((bf16[64,2,128]{2,0,1:T(8,128)(2,1)}), bf16[64,64,128]{2,0,1:T(8,128)(2,1)}) %all-gather.6.cloned.1.call-update) | async-done | bytes 1048592 | tf_op jit(solution)/shard_map/all_gather | solution.py:106
  198.6 3.4 gather_fusion.1
  202.0 5.8 convolution_bitcast_fusion.9
  207.7 3.8 fusion.129
  213.8 4.1 convolution_bitcast_fusion.8
  217.9 4.2 fusion.59
  222.1 3.0 copy.94
  225.1 78.4 %reduce-scatter.9.cloned.1.call-done = f32[64,2,128]{2,0,1:T(8,128)} async-done(((f32[64,64,128]{2,0,1:T(8,128)}), f32[64,2,128]{2,0,1:T(8,128)}) %reduce-scatter.9.cloned.1.call-update) | async-done | bytes 65552 | tf_op jit(solution)/shard_map/reduce_scatter | solution.py:95
  305.0 43.0 %all-gather.8.cloned.1.call-done = bf16[64,64,128]{2,0,1:T(8,128)(2,1)} async-done(((bf16[64,2,128]{2,0,1:T(8,128)(2,1)}), bf16[64,64,128]{2,0,1:T(8,128)(2,1)}) %all-gather.8.cloned.1.call-update) | async-done | bytes 1048592 | tf_op jit(solution)/shard_map/all_gather | solution.py:106
  348.0 3.4 gather_fusion.3
  351.3 5.8 convolution_bitcast_fusion.7
  357.1 3.8 fusion.126
  361.0 2.2 gather_fusion.4
  363.2 4.1 convolution_bitcast_fusion.6
  367.3 4.2 fusion.62
  371.4 2.7 copy.99
  374.2 78.4 %reduce-scatter.11.cloned.1.call-done = f32[64,2,128]{2,0,1:T(8,128)} async-done(((f32[64,64,128]{2,0,1:T(8,128)}), f32[64,2,128]{2,0,1:T(8,128)}) %reduce-scatter.11.cloned.1.call-update) | async-done | bytes 65552 | tf_op jit(solution)/shard_map/reduce_scatter | solution.py:95
  454.2 43.0 %all-gather.10.cloned.1.call-done = bf16[64,64,128]{2,0,1:T(8,128)(2,1)} async-done(((bf16[64,2,128]{2,0,1:T(8,128)(2,1)}), bf16[64,64,128]{2,0,1:T(8,128)(2,1)}) %all-gather.10.cloned.1.call-update) | async-done | bytes 1048592 | tf_op jit(solution)/shard_map/all_gather | solution.py:106
  497.1 3.4 gather_fusion.5
  500.5 5.7 convolution_bitcast_fusion.5
  506.2 3.8 fusion.123
  512.3 4.1 convolution_bitcast_fusion.4
  516.4 4.2 fusion.65
  520.6 3.0 copy.104
  523.6 78.4 %reduce-scatter.13.cloned.1.call-done = f32[64,2,128]{2,0,1:T(8,128)} async-done(((f32[64,64,128]{2,0,1:T(8,128)}), f32[64,2,128]{2,0,1:T(8,128)}) %reduce-scatter.13.cloned.1.call-update) | async-done | bytes 65552 | tf_op jit(solution)/shard_map/reduce_scatter | solution.py:95
  603.5 43.1 %all-gather.12.cloned.1.call-done = bf16[64,64,128]{2,0,1:T(8,128)(2,1)} async-done(((bf16[64,2,128]{2,0,1:T(8,128)(2,1)}), bf16[64,64,128]{2,0,1:T(8,128)(2,1)}) %all-gather.12.cloned.1.call-update) | async-done | bytes 1048592 | tf_op jit(solution)/shard_map/all_gather | solution.py:106
  646.6 3.4 gather_fusion.7
  650.0 5.8 convolution_bitcast_fusion.3
  655.8 3.8 fusion.120
  661.8 4.1 convolution_bitcast_fusion.2
  665.9 4.2 fusion.68
  670.1 2.7 copy.109
  672.9 78.4 %reduce-scatter.15.cloned.1.call-done = f32[64,2,128]{2,0,1:T(8,128)} async-done(((f32[64,64,128]{2,0,1:T(8,128)}), f32[64,2,128]{2,0,1:T(8,128)}) %reduce-scatter.15.cloned.1.call-update) | async-done | bytes 65552 | tf_op jit(solution)/shard_map/reduce_scatter | solution.py:95
  752.8 43.0 %all-gather.14.cloned.1.call-done = bf16[64,64,128]{2,0,1:T(8,128)(2,1)} async-done(((bf16[64,2,128]{2,0,1:T(8,128)(2,1)}), bf16[64,64,128]{2,0,1:T(8,128)(2,1)}) %all-gather.14.cloned.1.call-update) | async-done | bytes 1048592 | tf_op jit(solution)/shard_map/all_gather | solution.py:106
  795.8 3.4 gather_fusion.9
  799.1 5.8 convolution_bitcast_fusion.1
  804.9 3.8 fusion.213
  811.0 4.1 convolution_bitcast_fusion
  815.1 4.2 fusion.71
  819.2 2.8 copy.114
  824.1 76.3 %reduce-scatter.17.cloned.1.call-done = f32[64,2,128]{2,0,1:T(8,128)} async-done(((f32[64,64,128]{2,0,1:T(8,128)}), f32[64,2,128]{2,0,1:T(8,128)}) %reduce-scatter.17.cloned.1.call-update) | async-done | bytes 65552 | tf_op jit(solution)/shard_map/reduce_scatter | solution.py:95
  903.4 102.1 %all-reduce.3.cloned.1.call-done = f32[64,512]{1,0:T(8,128)} async-done(((f32[64,512]{1,0:T(8,128)}), f32[64,512]{1,0:T(8,128)}) %all-reduce.3.cloned.1.call-update) | async-done | bytes 131088 | tf_op jit(solution)/shard_map/psum | solution.py:112
  1006.8 17.3 %psum.15 = f32[16,512]{1,0:T(8,128)S(1)} all-reduce(f32[16,512]{1,0:T(8,128)S(1)} %fusion.162), channel_id=1, replica_groups=mesh['tiles'=32,'reps'=4] {'reps'}, use_global_device_ids=true, to_apply=%region_11.14 | all-reduce | flops 8192 | bytes 65536 | tf_op jit(solution)/shard_map/psum | solution.py:118
  (89 shorter events, 32.5 us)
Async XLA Ops:
  7.2 814.9 %copy-start = (f32[512,512]{1,0:T(8,128)S(1)}, f32[512,512]{1,0:T(8,128)}, u32[]{:S(2)}) copy-start(f32[512,512]{1,0:T(8,128)} %param.29) | copy-start | bytes 3145732
  7.2 3.1 copy-start.11
  7.2 3.1 copy-start.6
  7.2 131.7 %reduce-scatter.7.cloned.1.call-start = ((), (), s32[]{:S(2)}) async-start(), calls=%async_computation.6 | async-start | bytes 2162688 | tf_op jit(solution)/shard_map/reduce_scatter | solution.py:95
  23.3 0.7 copy-start.12
  23.4 175.2 %all-gather.6.cloned.1.call-start = ((), (), s32[]{:S(2)}) async-start(), calls=%async_computation.7 | async-start | bytes 1081344 | tf_op jit(solution)/shard_map/all_gather | solution.py:106
  25.2 113.4 %copy-start.7 = (s32[64,256]{1,0:T(8,128)S(1)}, s32[64,256]{1,0:T(8,128)}, u32[]{:S(2)}) copy-start(s32[64,256]{1,0:T(8,128)} %param.27) | copy-start | bytes 196612
  25.2 113.4 %copy-start.8 = (s32[256]{0:T(256)S(1)}, s32[256]{0:T(256)}, u32[]{:S(2)}) copy-start(s32[256]{0:T(256)} %param.26) | copy-start | bytes 3076
  25.2 113.4 %copy-start.9 = (f32[256]{0:T(256)S(1)}, f32[256]{0:T(256)}, u32[]{:S(2)}) copy-start(f32[256]{0:T(256)} %param.25) | copy-start | bytes 3076
  25.3 113.4 %copy-start.10 = (f32[256]{0:T(256)S(1)}, f32[256]{0:T(256)}, u32[]{:S(2)}) copy-start(f32[256]{0:T(256)} %param.24) | copy-start | bytes 3076
  25.3 115.4 %copy-start.5 = (s32[128]{0:T(128)S(1)}, s32[128]{0:T(128)}, u32[]{:S(2)}) copy-start(s32[128]{0:T(128)} %param.18) | copy-start | bytes 1540
  140.4 163.1 %reduce-scatter.9.cloned.1.call-start = ((), (), s32[]{:S(2)}) async-start(), calls=%async_computation.8 | async-start | bytes 2162688 | tf_op jit(solution)/shard_map/reduce_scatter | solution.py:95
  225.0 122.9 %all-gather.8.cloned.1.call-start = ((), (), s32[]{:S(2)}) async-start(), calls=%async_computation.9 | async-start | bytes 1081344 | tf_op jit(solution)/shard_map/all_gather | solution.py:106
  305.0 147.6 %reduce-scatter.11.cloned.1.call-start = ((), (), s32[]{:S(2)}) async-start(), calls=%async_computation.10 | async-start | bytes 2162688 | tf_op jit(solution)/shard_map/reduce_scatter | solution.py:95
  374.2 78.4 %copy-start.2 = (f32[64,2,128]{2,0,1:T(8,128)S(1)}, f32[64,2,128]{2,0,1:T(8,128)}, u32[]{:S(2)}) copy-start(f32[64,2,128]{2,0,1:T(8,128)} %reduce-scatter.7.cloned.1.call-done) | copy-start | bytes 196612
  374.2 122.9 %all-gather.10.cloned.1.call-start = ((), (), s32[]{:S(2)}) async-start(), calls=%async_computation.11 | async-start | bytes 1081344 | tf_op jit(solution)/shard_map/all_gather | solution.py:106
  454.1 147.9 %reduce-scatter.13.cloned.1.call-start = ((), (), s32[]{:S(2)}) async-start(), calls=%async_computation.12 | async-start | bytes 2162688 | tf_op jit(solution)/shard_map/reduce_scatter | solution.py:95
  523.5 78.4 %copy-start.3 = (f32[64,2,128]{2,0,1:T(8,128)S(1)}, f32[64,2,128]{2,0,1:T(8,128)}, u32[]{:S(2)}) copy-start(f32[64,2,128]{2,0,1:T(8,128)} %reduce-scatter.9.cloned.1.call-done) | copy-start | bytes 196612
  523.6 123.1 %all-gather.12.cloned.1.call-start = ((), (), s32[]{:S(2)}) async-start(), calls=%async_computation.13 | async-start | bytes 1081344 | tf_op jit(solution)/shard_map/all_gather | solution.py:106
  603.5 147.8 %reduce-scatter.15.cloned.1.call-start = ((), (), s32[]{:S(2)}) async-start(), calls=%async_computation.14 | async-start | bytes 2162688 | tf_op jit(solution)/shard_map/reduce_scatter | solution.py:95
  672.9 122.9 %all-gather.14.cloned.1.call-start = ((), (), s32[]{:S(2)}) async-start(), calls=%async_computation.15 | async-start | bytes 1081344 | tf_op jit(solution)/shard_map/all_gather | solution.py:106
  752.8 147.7 %reduce-scatter.17.cloned.1.call-start = ((), (), s32[]{:S(2)}) async-start(), calls=%async_computation.16 | async-start | bytes 2162688 | tf_op jit(solution)/shard_map/reduce_scatter | solution.py:95
  822.0 1.0 copy-start.1
  822.0 183.5 %all-reduce.3.cloned.1.call-start = ((), (), s32[]{:S(2)}) async-start(), calls=%async_computation.17 | async-start | bytes 262144 | tf_op jit(solution)/shard_map/psum | solution.py:112
  901.3 124.9 %copy-start.4 = (f32[64,256]{1,0:T(8,128)}, f32[64,256]{1,0:T(8,128)S(1)}, u32[]{:S(2)}) copy-start(f32[64,256]{1,0:T(8,128)S(1)} %copy_bitcast_fusion.1) | copy-start | bytes 196612
Sparse Core Ops, SparseCore 0:
  23.5 80.7 reduce-scatter.6
  140.5 58.0 all-gather.5
  225.2 78.2 reduce-scatter.8
  306.1 41.7 all-gather.7
  374.3 78.2 reduce-scatter.10
  455.3 41.7 all-gather.9
  523.7 78.2 reduce-scatter.12
  604.8 41.7 all-gather.11
  673.0 78.2 reduce-scatter.14
  753.9 41.7 all-gather.13
  822.2 78.2 reduce-scatter.16
  904.1 101.3 all-reduce.2
where the time goes:
time: 1040 us; the launch traced here: 1030 us
  waiting for transfers between devices  722 us (69%)
  blocking collectives  127 us (12%)
  matrix products  103 us (10%)
  local copies, waits for them, and re-layouts  51.7 us (5%)
  between operations  15.5 us (1%)
  other arithmetic  13.9 us (1%)
    reduce_scatter x6, waiting for transfers between devices, body(): lax.psum_scatter(jnp.einsum('nt,rtf->rnf', dense_hot, pushed, precision=h...  390 us
    all_gather x5, waiting for transfers between devices, body(): every_firm = lax.all_gather(firm_round, 'tiles', axis=1, tiled=True)  230 us
    unnamed x1, blocking collectives  110 us
    psum x1, waiting for transfers between devices, body(): summed = lax.psum(local_term, 'tiles')  102 us
    dot_general x5, matrix products, body(): jnp.einsum('twf,rtf->rtw', tiles_w, tile_firm, preferred_element_type=jnp...  28.7 us
    dot_general x6, matrix products, body(): jnp.einsum('nt,rtf->rnf', dense_hot, pushed, precision=highest)  24.9 us
    dot_general x6, matrix products, body(): jnp.einsum('twf,rtw->rtf', tiles_w, tile_values, preferred_element_type=j...  24.6 us
  transfers between devices with their start and end apart: 12, of which 11 were waited for; matrix products, arithmetic and copies ran while one was open for 1% of the time, Pallas kernels for 0%

commit v1 on v0

--- a/solution.py
+++ b/solution.py
@@ -103,7 +103,7 @@
         firm_older, firm_newer = (firm_newer, firm_now)
         if sweep_index + 1 < SWEEPS:
             firm_round = firm_now.astype(jnp.bfloat16)
-            every_firm = lax.all_gather(firm_round, "tiles", axis=1, tiled=True)
+            every_firm = jnp.concatenate(lax.all_gather(firm_round, "tiles"), axis=1)
             tile_firm = jnp.take(every_firm, tile_block, axis=1)
     worker_effect = worker_now.reshape(replicas_here, WORK_BLOCKS * tile_cells)
     firm_flat = firm_now.reshape(replicas_here, FIRM_BLOCKS * tile_cells)

time: 1040 us -> 1040 us (level)
  no operation moved by 1% of the time
where the time goes in v1:
time: 1040 us; the launch traced here: 1030 us
  waiting for transfers between devices  722 us (69%)
  blocking collectives  127 us (12%)
  matrix products  103 us (10%)
  local copies, waits for them, and re-layouts  56.1 us (5%)
  between operations  15.6 us (2%)
  other arithmetic  10.8 us (1%)
    reduce_scatter x6, waiting for transfers between devices, body(): lax.psum_scatter(jnp.einsum('nt,rtf->rnf', dense_hot, pushed, precision=h...  390 us
    all_gather x5, waiting for transfers between devices, body(): every_firm = jnp.concatenate(lax.all_gather(firm_round, 'tiles'), axis=1)  230 us
    unnamed x1, blocking collectives  110 us
    psum x1, waiting for transfers between devices, body(): summed = lax.psum(local_term, 'tiles')  102 us
    dot_general x5, matrix products, body(): jnp.einsum('twf,rtf->rtw', tiles_w, tile_firm, preferred_element_type=jnp...  28.8 us
    dot_general x6, matrix products, body(): jnp.einsum('nt,rtf->rnf', dense_hot, pushed, precision=highest)  24.9 us
    dot_general x6, matrix products, body(): jnp.einsum('twf,rtw->rtf', tiles_w, tile_values, preferred_element_type=j...  24.6 us
  transfers between devices with their start and end apart: 12, of which 11 were waited for; matrix products, arithmetic and copies ran while one was open for 1% of the time, Pallas kernels for 0%

profile of v1, /device:TPU:6, one launch (start us, length us, event | category | flops | bytes accessed | tf_op | source)
XLA Modules:
  0.0 1034.6 jit_solution(8647276553938843925)
XLA Ops:
  12.5 4.1 convolution_bitcast_fusion.10
  16.6 4.2 fusion.56
  20.8 2.6 copy.109
  25.3 3.5 convert_reduce_fusion
  28.9 109.8 %all-reduce = f32[64,128]{1,0:T(8,128)S(1)} all-reduce(f32[64,128]{1,0:T(8,128)S(1)} %fusion.164), channel_id=8, replica_groups=mesh['tiles'=32,'reps'=4] {'tiles'}, use_global_device_ids=true, to_apply=%region_3.0.clone | all-reduce | flops 8192 | bytes 65536
  140.8 57.8 %all-gather.11.cloned.1.call-done = bf16[2048,2,128]{2,1,0:T(2,128)(2,1)} async-done(((bf16[64,2,128]{2,1,0:T(2,128)(2,1)}), bf16[2048,2,128]{2,1,0:T(2,128)(2,1)}) %all-gather.11.cloned.1.call-update) | async-done | bytes 1048592 | tf_op jit(solution)/shard_map/all_gather | solution.py:106
  200.1 2.2 gather_fusion.1
  202.3 5.8 convolution_bitcast_fusion.9
  208.0 3.8 fusion.129
  211.9 2.2 gather_fusion.2
  214.1 4.1 convolution_bitcast_fusion.8
  218.2 4.2 fusion.59
  222.3 3.0 copy.117
  225.4 78.3 %reduce-scatter.9.cloned.1.call-done = f32[64,2,128]{2,0,1:T(8,128)} async-done(((f32[64,64,128]{2,0,1:T(8,128)}), f32[64,2,128]{2,0,1:T(8,128)}) %reduce-scatter.9.cloned.1.call-update) | async-done | bytes 65552 | tf_op jit(solution)/shard_map/reduce_scatter | solution.py:95
  305.3 43.0 %all-gather.13.cloned.1.call-done = bf16[2048,2,128]{2,1,0:T(2,128)(2,1)} async-done(((bf16[64,2,128]{2,1,0:T(2,128)(2,1)}), bf16[2048,2,128]{2,1,0:T(2,128)(2,1)}) %all-gather.13.cloned.1.call-update) | async-done | bytes 1048592 | tf_op jit(solution)/shard_map/all_gather | solution.py:106
  349.7 2.2 gather_fusion.3
  351.9 5.8 convolution_bitcast_fusion.7
  357.6 3.8 fusion.126
  363.7 4.1 convolution_bitcast_fusion.6
  367.8 4.2 fusion.62
  372.0 2.7 copy.125
  374.8 78.3 %reduce-scatter.11.cloned.1.call-done = f32[64,2,128]{2,0,1:T(8,128)} async-done(((f32[64,64,128]{2,0,1:T(8,128)}), f32[64,2,128]{2,0,1:T(8,128)}) %reduce-scatter.11.cloned.1.call-update) | async-done | bytes 65552 | tf_op jit(solution)/shard_map/reduce_scatter | solution.py:95
  454.7 42.9 %all-gather.15.cloned.1.call-done = bf16[2048,2,128]{2,1,0:T(2,128)(2,1)} async-done(((bf16[64,2,128]{2,1,0:T(2,128)(2,1)}), bf16[2048,2,128]{2,1,0:T(2,128)(2,1)}) %all-gather.15.cloned.1.call-update) | async-done | bytes 1048592 | tf_op jit(solution)/shard_map/all_gather | solution.py:106
  499.1 2.2 gather_fusion.5
  501.3 5.8 convolution_bitcast_fusion.5
  507.0 3.8 fusion.123
  513.1 4.1 convolution_bitcast_fusion.4
  517.2 4.2 fusion.65
  521.3 3.0 copy.133
  524.4 78.4 %reduce-scatter.13.cloned.1.call-done = f32[64,2,128]{2,0,1:T(8,128)} async-done(((f32[64,64,128]{2,0,1:T(8,128)}), f32[64,2,128]{2,0,1:T(8,128)}) %reduce-scatter.13.cloned.1.call-update) | async-done | bytes 65552 | tf_op jit(solution)/shard_map/reduce_scatter | solution.py:95
  604.3 43.1 %all-gather.17.cloned.1.call-done = bf16[2048,2,128]{2,1,0:T(2,128)(2,1)} async-done(((bf16[64,2,128]{2,1,0:T(2,128)(2,1)}), bf16[2048,2,128]{2,1,0:T(2,128)(2,1)}) %all-gather.17.cloned.1.call-update) | async-done | bytes 1048592 | tf_op jit(solution)/shard_map/all_gather | solution.py:106
  648.9 2.2 gather_fusion.7
  651.0 5.8 convolution_bitcast_fusion.3
  656.8 3.8 fusion.120
  662.9 4.1 convolution_bitcast_fusion.2
  667.0 4.2 fusion.68
  671.1 2.7 copy.141
  673.9 78.4 %reduce-scatter.15.cloned.1.call-done = f32[64,2,128]{2,0,1:T(8,128)} async-done(((f32[64,64,128]{2,0,1:T(8,128)}), f32[64,2,128]{2,0,1:T(8,128)}) %reduce-scatter.15.cloned.1.call-update) | async-done | bytes 65552 | tf_op jit(solution)/shard_map/reduce_scatter | solution.py:95
  753.9 42.9 %all-gather.19.cloned.1.call-done = bf16[2048,2,128]{2,1,0:T(2,128)(2,1)} async-done(((bf16[64,2,128]{2,1,0:T(2,128)(2,1)}), bf16[2048,2,128]{2,1,0:T(2,128)(2,1)}) %all-gather.19.cloned.1.call-update) | async-done | bytes 1048592 | tf_op jit(solution)/shard_map/all_gather | solution.py:106
  798.2 2.2 gather_fusion.9
  800.4 5.8 convolution_bitcast_fusion.1
  806.2 3.8 fusion.213
  812.2 4.1 convolution_bitcast_fusion
  816.3 4.2 fusion.71
  820.5 2.8 copy.149
  825.4 76.3 %reduce-scatter.17.cloned.1.call-done = f32[64,2,128]{2,0,1:T(8,128)} async-done(((f32[64,64,128]{2,0,1:T(8,128)}), f32[64,2,128]{2,0,1:T(8,128)}) %reduce-scatter.17.cloned.1.call-update) | async-done | bytes 65552 | tf_op jit(solution)/shard_map/reduce_scatter | solution.py:95
  904.6 102.2 %all-reduce.3.cloned.1.call-done = f32[64,512]{1,0:T(8,128)} async-done(((f32[64,512]{1,0:T(8,128)}), f32[64,512]{1,0:T(8,128)}) %all-reduce.3.cloned.1.call-update) | async-done | bytes 131088 | tf_op jit(solution)/shard_map/psum | solution.py:112
  1008.1 17.3 %psum.15 = f32[16,512]{1,0:T(8,128)S(1)} all-reduce(f32[16,512]{1,0:T(8,128)S(1)} %fusion.162), channel_id=1, replica_groups=mesh['tiles'=32,'reps'=4] {'reps'}, use_global_device_ids=true, to_apply=%region_11.14 | all-reduce | flops 8192 | bytes 65536 | tf_op jit(solution)/shard_map/psum | solution.py:118
  (104 shorter events, 40.0 us)
Async XLA Ops:
  7.2 816.2 %copy-start = (f32[512,512]{1,0:T(8,128)S(1)}, f32[512,512]{1,0:T(8,128)}, u32[]{:S(2)}) copy-start(f32[512,512]{1,0:T(8,128)} %param.29) | copy-start | bytes 3145732
  7.2 3.1 copy-start.11
  7.2 3.1 copy-start.6
  7.2 131.7 %reduce-scatter.7.cloned.1.call-start = ((), (), s32[]{:S(2)}) async-start(), calls=%async_computation.6 | async-start | bytes 2162688 | tf_op jit(solution)/shard_map/reduce_scatter | solution.py:95
  23.3 0.7 copy-start.12
  23.4 175.3 %all-gather.11.cloned.1.call-start = ((), (), s32[]{:S(2)}) async-start(), calls=%async_computation.13 | async-start | bytes 1081344 | tf_op jit(solution)/shard_map/all_gather | solution.py:106
  25.2 113.5 %copy-start.7 = (s32[64,256]{1,0:T(8,128)S(1)}, s32[64,256]{1,0:T(8,128)}, u32[]{:S(2)}) copy-start(s32[64,256]{1,0:T(8,128)} %param.27) | copy-start | bytes 196612
  25.2 113.5 %copy-start.8 = (s32[256]{0:T(256)S(1)}, s32[256]{0:T(256)}, u32[]{:S(2)}) copy-start(s32[256]{0:T(256)} %param.26) | copy-start | bytes 3076
  25.2 113.5 %copy-start.9 = (f32[256]{0:T(256)S(1)}, f32[256]{0:T(256)}, u32[]{:S(2)}) copy-start(f32[256]{0:T(256)} %param.25) | copy-start | bytes 3076
  25.3 113.5 %copy-start.10 = (f32[256]{0:T(256)S(1)}, f32[256]{0:T(256)}, u32[]{:S(2)}) copy-start(f32[256]{0:T(256)} %param.24) | copy-start | bytes 3076
  25.3 115.4 %copy-start.5 = (s32[128]{0:T(128)S(1)}, s32[128]{0:T(128)}, u32[]{:S(2)}) copy-start(s32[128]{0:T(128)} %param.18) | copy-start | bytes 1540
  140.4 163.3 %reduce-scatter.9.cloned.1.call-start = ((), (), s32[]{:S(2)}) async-start(), calls=%async_computation.7 | async-start | bytes 2162688 | tf_op jit(solution)/shard_map/reduce_scatter | solution.py:95
  225.3 122.9 %all-gather.13.cloned.1.call-start = ((), (), s32[]{:S(2)}) async-start(), calls=%async_computation.14 | async-start | bytes 1081344 | tf_op jit(solution)/shard_map/all_gather | solution.py:106
  305.2 147.8 %reduce-scatter.11.cloned.1.call-start = ((), (), s32[]{:S(2)}) async-start(), calls=%async_computation.8 | async-start | bytes 2162688 | tf_op jit(solution)/shard_map/reduce_scatter | solution.py:95
  374.7 78.4 %copy-start.2 = (f32[64,2,128]{2,0,1:T(8,128)S(1)}, f32[64,2,128]{2,0,1:T(8,128)}, u32[]{:S(2)}) copy-start(f32[64,2,128]{2,0,1:T(8,128)} %reduce-scatter.7.cloned.1.call-done) | copy-start | bytes 196612
  374.7 122.9 %all-gather.15.cloned.1.call-start = ((), (), s32[]{:S(2)}) async-start(), calls=%async_computation.15 | async-start | bytes 1081344 | tf_op jit(solution)/shard_map/all_gather | solution.py:106
  454.6 148.1 %reduce-scatter.13.cloned.1.call-start = ((), (), s32[]{:S(2)}) async-start(), calls=%async_computation.9 | async-start | bytes 2162688 | tf_op jit(solution)/shard_map/reduce_scatter | solution.py:95
  524.3 78.4 %copy-start.3 = (f32[64,2,128]{2,0,1:T(8,128)S(1)}, f32[64,2,128]{2,0,1:T(8,128)}, u32[]{:S(2)}) copy-start(f32[64,2,128]{2,0,1:T(8,128)} %reduce-scatter.9.cloned.1.call-done) | copy-start | bytes 196612
  524.3 123.1 %all-gather.17.cloned.1.call-start = ((), (), s32[]{:S(2)}) async-start(), calls=%async_computation.16 | async-start | bytes 1081344 | tf_op jit(solution)/shard_map/all_gather | solution.py:106
  604.3 148.0 %reduce-scatter.15.cloned.1.call-start = ((), (), s32[]{:S(2)}) async-start(), calls=%async_computation.10 | async-start | bytes 2162688 | tf_op jit(solution)/shard_map/reduce_scatter | solution.py:95
  673.9 122.9 %all-gather.19.cloned.1.call-start = ((), (), s32[]{:S(2)}) async-start(), calls=%async_computation.17 | async-start | bytes 1081344 | tf_op jit(solution)/shard_map/all_gather | solution.py:106
  753.8 147.9 %reduce-scatter.17.cloned.1.call-start = ((), (), s32[]{:S(2)}) async-start(), calls=%async_computation.11 | async-start | bytes 2162688 | tf_op jit(solution)/shard_map/reduce_scatter | solution.py:95
  823.3 1.0 copy-start.1
  823.3 183.5 %all-reduce.3.cloned.1.call-start = ((), (), s32[]{:S(2)}) async-start(), calls=%async_computation.12 | async-start | bytes 262144 | tf_op jit(solution)/shard_map/psum | solution.py:112
  902.6 125.0 %copy-start.4 = (f32[64,256]{1,0:T(8,128)}, f32[64,256]{1,0:T(8,128)S(1)}, u32[]{:S(2)}) copy-start(f32[64,256]{1,0:T(8,128)S(1)} %copy_bitcast_fusion.1) | copy-start | bytes 196612
Sparse Core Ops, SparseCore 0:
  23.5 80.8 reduce-scatter.6
  140.6 58.0 all-gather.10
  225.5 78.2 reduce-scatter.8
  306.4 41.8 all-gather.12
  374.8 78.2 reduce-scatter.10
  455.8 41.8 all-gather.14
  524.5 78.2 reduce-scatter.12
  605.6 41.7 all-gather.16
  674.0 78.2 reduce-scatter.14
  755.0 41.7 all-gather.18
  823.4 78.2 reduce-scatter.16
  905.3 101.4 all-reduce.2
